TPU v7x, 32 devices: a whole 2x2x4 slice. The times are simulated.
32 devices in a mesh: head: 4 (over y, x), blk: 8 (over z, core).
Axes of the slice: x: 2, y: 2, z: 4, core: 2. Of those that a mesh axis runs over, the one named last changes fastest.
Arguments:
- hidden_in: bfloat16 [2048, 4096], P(('blk', 'head')), may hold values from -6 to 6
- queries: bfloat16 [2048, 2048], P(('blk', 'head')), may hold values from -26 to 26
- key_states: bfloat16 [2048, 1024], P(('blk', 'head')), may hold values from -5 to 5
- value_states: bfloat16 [2048, 1024], P(('blk', 'head')), may hold values from -6 to 6
- out_weight: bfloat16 [2048, 4096], P('head'), may hold values from -0.125 to 0.125
- norm_gain: float32 [4096], replicated, may hold values from 0.1 to 1.9
- gate_weight: bfloat16 [4096, 7168], P(None, 'head'), may hold values from -0.09375 to 0.09375
- up_weight: bfloat16 [4096, 7168], P(None, 'head'), may hold values from -0.09375 to 0.09375
- down_weight: bfloat16 [7168, 4096], P('head'), may hold values from -0.0625 to 0.0625
Outputs:
- layer_out: bfloat16 [2048, 4096], P(('blk', 'head'))
All inputs are finite; a program needn't handle non-finite values.
Results may differ from a plain program's by a relative error of at most 0.018.
Values may be sent and summed in bfloat16 or wider, within the bound.
A program may use at most 192 MiB of HBM per device.

v0:
```python
import jax
import jax.numpy as jnp
from jax import lax
from jax.sharding import PartitionSpec as P

HEADS = 16
KV_HEADS = 8
HEAD_DIM = 128


negative_fill = -1e30


def absorb_rows(running, query_groups, query_pos, key_block, value_block, key_pos):
    row_peak, row_total, weighted = running
    key_count = key_block.shape[0]
    group_count = query_groups.shape[1]
    head_size = query_groups.shape[3]
    key_heads = key_block.reshape(key_count, group_count, head_size)
    value_heads = value_block.reshape(key_count, group_count, head_size)
    scores = jnp.einsum(
        "qgrd,kgd->grqk", query_groups, key_heads, preferred_element_type=jnp.float32
    ) * head_size ** (-0.5)
    visible = key_pos[None, :] <= query_pos[:, None]
    new_peak = jnp.maximum(row_peak, jnp.max(jnp.where(visible, scores, negative_fill), axis=-1))
    exp_scores = jnp.where(visible, jnp.exp(scores - new_peak[..., None]), 0.0)
    new_total = jnp.sum(exp_scores, axis=-1)
    products = jnp.einsum(
        "grqk,kgd->grqd",
        exp_scores.astype(jnp.bfloat16),
        value_heads,
        preferred_element_type=jnp.float32,
    )
    return (new_peak, new_total, products)


def local(
    hidden_in,
    queries,
    key_states,
    value_states,
    out_weight,
    norm_gain,
    gate_weight,
    up_weight,
    down_weight,
):
    own_block = lax.axis_index("blk")
    query_local, key_local, value_local = (
        lax.all_to_all(queries, "head", split_axis=1, concat_axis=0, tiled=True),
        lax.all_to_all(key_states, "head", split_axis=1, concat_axis=0, tiled=True),
        lax.all_to_all(value_states, "head", split_axis=1, concat_axis=0, tiled=True),
    )
    block_rows = query_local.shape[0]
    query_width = query_local.shape[1]
    key_width = key_local.shape[1]
    group_count = key_width // HEAD_DIM
    group_ratio = HEADS // KV_HEADS
    local_index = jnp.arange(block_rows, dtype=jnp.int32)
    start_state = (
        jnp.full((group_count, group_ratio, block_rows), negative_fill, jnp.float32),
        jnp.zeros((group_count, group_ratio, block_rows), jnp.float32),
        jnp.zeros((group_count, group_ratio, block_rows, HEAD_DIM), jnp.float32),
    )
    query_pos = own_block * block_rows + local_index
    query_groups = query_local.reshape(block_rows, group_count, group_ratio, HEAD_DIM)
    last_query = own_block * block_rows + block_rows - 1
    key_block = lax.all_gather(key_local, "blk", axis=0, tiled=True)
    value_block = lax.all_gather(value_local, "blk", axis=0, tiled=True)
    key_pos = jnp.arange(key_block.shape[0], dtype=jnp.int32)

    def skipped(state):
        return state

    def worked(state):
        return absorb_rows(state, query_groups, query_pos, key_block, value_block, key_pos)

    row_peak, row_total, weighted = lax.cond(
        jnp.int32(0) > last_query, skipped, worked, start_state
    )
    attended = (
        (weighted / row_total[..., None])
        .transpose(2, 0, 1, 3)
        .reshape(block_rows, query_width)
        .astype(jnp.bfloat16)
    )
    selected = attended
    projected = lax.psum_scatter(
        jnp.dot(selected, out_weight, preferred_element_type=jnp.float32).astype(jnp.bfloat16),
        "head",
        scatter_dimension=0,
        tiled=True,
    ).astype(jnp.float32)
    residual = (hidden_in.astype(jnp.float32) + projected).astype(jnp.bfloat16)
    widened = residual.astype(jnp.float32)
    mean_square = jnp.mean(widened * widened, axis=-1, keepdims=True)
    normed = (widened * lax.rsqrt(mean_square + 1e-05) * norm_gain).astype(jnp.bfloat16)
    shard_rows = lax.all_gather(normed, "head", axis=0, tiled=True)
    gate_part = jnp.dot(shard_rows, gate_weight, preferred_element_type=jnp.float32)
    up_part = jnp.dot(shard_rows, up_weight, preferred_element_type=jnp.float32)
    inner_act = (jax.nn.silu(gate_part) * up_part).astype(jnp.bfloat16)
    selected = inner_act
    mlp_out = lax.psum_scatter(
        jnp.dot(selected, down_weight, preferred_element_type=jnp.float32).astype(jnp.bfloat16),
        "head",
        scatter_dimension=0,
        tiled=True,
    ).astype(jnp.float32)
    return (residual.astype(jnp.float32) + mlp_out).astype(jnp.bfloat16)


def solution(mesh):
    return jax.shard_map(
        local,
        mesh=mesh,
        in_specs=(
            P(("blk", "head"), None),
            P(("blk", "head"), None),
            P(("blk", "head"), None),
            P(("blk", "head"), None),
            P("head", None),
            P(),
            P(None, "head"),
            P(None, "head"),
            P("head", None),
        ),
        out_specs=P(("blk", "head"), None),
        check_vma=False,
    )
```

profile of v0, /device:TPU:24, one launch (start us, length us, event | category | flops | bytes accessed | tf_op | source)
XLA Modules:
  0.0 229.2 jit_solution(15140094676042932576)
XLA Ops:
  6.5 0.0 all-gather.4.cloned.1.call-start
  6.5 0.9 copy.59
  7.5 8.6 %all_to_all.54 = bf16[64,4,256]{2,0,1:T(8,128)(2,1)} all-to-all(bf16[64,4,256]{2,0,1:T(8,128)(2,1)S(1)} %bitcast.51), channel_id=1, replica_groups=mesh['head'=4,'blk'=8] {'head'}, dimensions={1} | all-to-all | bytes 262144 | tf_op jit(solution)/shard_map/all_to_all | solution.py:51
  16.1 0.0 all-gather.4.cloned.1.call-update
  16.1 0.0 all-gather.6.cloned.1.call-start
  16.2 0.9 copy.58
  17.1 8.1 %all_to_all.55 = bf16[64,4,256]{2,0,1:T(8,128)(2,1)} all-to-all(bf16[64,4,256]{2,0,1:T(8,128)(2,1)S(1)} %bitcast.52), channel_id=1, replica_groups=mesh['head'=4,'blk'=8] {'head'}, dimensions={1} | all-to-all | bytes 262144 | tf_op jit(solution)/shard_map/all_to_all | solution.py:52
  25.2 0.0 all-gather.6.cloned.1.call-update
  25.2 1.7 copy.57
  26.9 3.4 %all-to-all-start.1 = ((bf16[64,4,512]{2,0,1:T(8,128)(2,1)}), bf16[64,4,512]{2,0,1:T(8,128)(2,1)S(1)}, u32[]{:S(2)}, u32[]{:S(2)}) async-start(bf16[64,4,512]{2,0,1:T(8,128)(2,1)} %bitcast.42), calls=%async_computation.1 | async-start | bytes 524288 | tf_op jit(solution)/shard_map/all_to_all | solution.py:50
  30.3 0.0 reduce-scatter.3.cloned.1.call-start
  30.3 5.3 %all-to-all-done.1 = bf16[64,4,512]{2,0,1:T(8,128)(2,1)S(1)} async-done(((bf16[64,4,512]{2,0,1:T(8,128)(2,1)}), bf16[64,4,512]{2,0,1:T(8,128)(2,1)S(1)}, u32[]{:S(2)}, u32[]{:S(2)}) %all-to-all-start.1) | async-done | bytes 262176 | tf_op jit(solution)/shard_map/all_to_all | solution.py:50
  35.6 1.1 all-gather.4.cloned.1.call-done
  36.7 23.5 %all-gather.6.cloned.1.call-done = bf16[2048,256]{1,0:T(8,128)(2,1)} async-done(((bf16[256,256]{1,0:T(8,128)(2,1)}), bf16[2048,256]{1,0:T(8,128)(2,1)}) %all-gather.6.cloned.1.call-update) | async-done | bytes 1048592 | tf_op jit(solution)/shard_map/all_gather | solution.py:69
  60.2 14.5 %conditional.1 = (f32[2,2,256]{2,1,0:T(2,128)S(1)}, f32[2,2,256,128]{2,3,1,0:T(8,128)S(1)}) conditional(s32[]{:T(128)} %convert_element_type.47, (s32[2048]{0:T(1024)S(1)}, s32[]{:T(128)}, s32[256]{0:T(256)S(1)}, bf16[2048,256]{1,0:T(8,128)(2,1)}, bf16[4,64,512]{2,1,0:T(8,128)(2,1)S(1)}, /*index=5*/bf16[2048,256]{1,0:T(8,128)(2,1)}) %tuple.31, () %tuple.14), branch_computations={%region_0.3_spmd, %region_3.4_spmd} | conditional | flops 1097334016 | bytes 72649808 | solution.py:78
  60.2 0.4 broadcast_compare_fusion
  60.6 1.3 reshape.34
  62.0 0.1 reshape.35
  62.1 0.0 copy-start.3
  62.1 4.7 %fusion = (f32[2,2,256]{2,1,0:T(2,128)S(1)}, f32[2,2048,256,2]{2,1,3,0:T(8,128)}) fusion(pred[256,2048]{0,1:T(8,128)(4,1)S(1)} %broadcast_compare_fusion, bf16[256,2,2,128]{3,2,1,0:T(2,128)(2,1)S(1)} %reshape.35, bf16[2048,2,128,1]{2,1,0,3:T(2,128)(2,1)S(1)} %bitcast.46), kind=kOutput, calls=%fused_computation.2 | convolution fusion | flops 543161344 | bytes 10227712 | tf_op jit(solution)/shard_map/cond/branch_0_fun/qgrd,kgd->grqk/dot_general | solution.py:21
  66.8 0.0 copy-done.3
  66.8 0.3 reshape.36
  67.1 0.0 copy-start
  67.1 5.3 %fusion.5 = f32[2,2,256,128]{2,3,1,0:T(8,128)S(1)} fusion(f32[2,2048,256,2]{2,1,3,0:T(8,128)} %get-tuple-element.38, f32[2,2,256]{2,1,0:T(2,128)S(1)} %broadcast_maximum_fusion, pred[256,2048]{0,1:T(8,128)(4,1)S(1)} %broadcast_compare_fusion, bf16[2048,2,128,1]{2,1,0,3:T(2,128)(2,1)S(1)} %bitcast.47), kind=kOutput, calls=%fused_computation.7 | convolution fusion | flops 545259520 | bytes 10489856 | tf_op jit(solution)/shard_map/cond | solution.py:78
  72.4 0.4 copy-done
  72.9 1.8 fusion.4
  74.7 0.0 copy-start.1
  74.7 0.0 copy-start.4
  74.7 4.9 %convolution_convert_fusion.1 = bf16[256,4096]{1,0:T(8,128)(2,1)} fusion(bf16[256,512]{0,1:T(8,128)(2,1)S(1)} %bitcast.45, bf16[512,4096]{1,0:T(8,128)(2,1)} %param.15), kind=kOutput, calls=%fused_computation.19 | convolution fusion | flops 1074790400 | bytes 6553600 | tf_op jit(solution)/shard_map/dot_general | solution.py:89
  79.6 0.0 reduce-scatter.3.cloned.1.call-update
  79.6 0.0 all-gather.8.cloned.1.call-start
  79.7 36.1 %reduce-scatter.3.cloned.1.call-done = bf16[64,4096]{1,0:T(8,128)(2,1)} async-done(((bf16[256,4096]{1,0:T(8,128)(2,1)}), bf16[64,4096]{1,0:T(8,128)(2,1)}) %reduce-scatter.3.cloned.1.call-update) | async-done | bytes 524304 | tf_op jit(solution)/shard_map/reduce_scatter | solution.py:88
  115.8 0.0 copy-done.1
  115.8 1.3 fusion.15
  117.1 0.0 copy-done.4
  117.1 2.0 fusion.17
  119.2 0.0 all-gather.8.cloned.1.call-update
  119.2 0.2 reduce-scatter.5.cloned.1.call-start
  119.4 35.1 %all-gather.8.cloned.1.call-done = bf16[256,4096]{1,0:T(8,128)(2,1)} async-done(((bf16[64,4096]{1,0:T(8,128)(2,1)}), bf16[256,4096]{1,0:T(8,128)(2,1)}) %all-gather.8.cloned.1.call-update) | async-done | bytes 2097168 | tf_op jit(solution)/shard_map/all_gather | solution.py:98
  154.6 0.0 copy-start.5
  154.6 11.1 %fusion.20 = f32[256,1792]{1,0:T(8,128)} fusion(bf16[256,4096]{1,0:T(8,128)(2,1)} %all-gather.8.cloned.1.call-done, bf16[4096,1792]{1,0:T(8,128)(2,1)} %param.17), kind=kOutput, calls=%fused_computation.36 | convolution fusion | flops 3758096384 | bytes 18612224 | tf_op jit(solution)/shard_map/dot_general | solution.py:99
  165.7 0.0 copy-done.5
  165.7 0.0 copy-start.2
  165.7 19.6 %convolution_convert_fusion = bf16[256,4096]{1,0:T(8,128)(2,1)} fusion(bf16[1792,4096]{1,0:T(8,128)(2,1)} %param.19, bf16[256,4096]{1,0:T(8,128)(2,1)S(1)} %copy-done.5, bf16[4096,1792]{1,0:T(8,128)(2,1)} %param.18, f32[256,1792]{1,0:T(8,128)} %fusion.20), kind=kOutput, calls=%fused_computation.18 | convolution fusion | flops 7519993856 | bytes 35389440 | tf_op jit(solution)/shard_map/dot_general | solution.py:104
  185.3 0.0 reduce-scatter.5.cloned.1.call-update
  185.3 35.3 %reduce-scatter.5.cloned.1.call-done = bf16[64,4096]{1,0:T(8,128)(2,1)} async-done(((bf16[256,4096]{1,0:T(8,128)(2,1)}), bf16[64,4096]{1,0:T(8,128)(2,1)}) %reduce-scatter.5.cloned.1.call-update) | async-done | bytes 524304 | tf_op jit(solution)/shard_map/reduce_scatter | solution.py:103
  220.7 0.0 copy-done.2
  220.7 2.0 fusion.18
  (6 shorter events, 0.1 us)
Async XLA Ops:
  6.5 30.2 %all-gather.4.cloned.1.call-start = ((), (), s32[]{:S(2)}) async-start(), calls=%async_computation.5 | async-start | bytes 1179648 | tf_op jit(solution)/shard_map/all_gather | solution.py:68
  16.1 44.1 %all-gather.6.cloned.1.call-start = ((), (), s32[]{:S(2)}) async-start(), calls=%async_computation.6 | async-start | bytes 1179648 | tf_op jit(solution)/shard_map/all_gather | solution.py:69
  26.9 8.8 %all-to-all-start.1 = ((bf16[64,4,512]{2,0,1:T(8,128)(2,1)}), bf16[64,4,512]{2,0,1:T(8,128)(2,1)S(1)}, u32[]{:S(2)}, u32[]{:S(2)}) async-start(bf16[64,4,512]{2,0,1:T(8,128)(2,1)} %bitcast.42), calls=%async_computation.1 | async-start | bytes 524288 | tf_op jit(solution)/shard_map/all_to_all | solution.py:50
  30.3 85.5 %reduce-scatter.3.cloned.1.call-start = ((), (), s32[]{:S(2)}) async-start(), calls=%async_computation.7 | async-start | bytes 2621440 | tf_op jit(solution)/shard_map/reduce_scatter | solution.py:88
  62.1 4.7 %copy-start.3 = (bf16[2048,256]{1,0:T(8,128)(2,1)S(1)}, bf16[2048,256]{1,0:T(8,128)(2,1)}, u32[]{:S(2)}) copy-start(bf16[2048,256]{1,0:T(8,128)(2,1)} %get-tuple-element.25) | copy-start | bytes 3145732 | tf_op jit(solution)/shard_map/cond
  67.1 5.8 %copy-start = (f32[2,2048,256,2]{2,1,3,0:T(8,128)S(1)}, f32[2,2048,256,2]{2,1,3,0:T(8,128)}, u32[]{:S(2)}) copy-start(f32[2,2048,256,2]{2,1,3,0:T(8,128)} %get-tuple-element.38) | copy-start | bytes 25165828 | tf_op jit(solution)/shard_map/cond
  74.7 41.1 %copy-start.1 = (bf16[64,4096]{1,0:T(8,128)(2,1)S(1)}, bf16[64,4096]{1,0:T(8,128)(2,1)}, u32[]{:S(2)}) copy-start(bf16[64,4096]{1,0:T(8,128)(2,1)} %param.11) | copy-start | bytes 1572868
  74.7 42.4 %copy-start.4 = (f32[4096]{0:T(1024)S(1)}, f32[4096]{0:T(1024)}, u32[]{:S(2)}) copy-start(f32[4096]{0:T(1024)} %param.16) | copy-start | bytes 49156
  79.6 74.9 %all-gather.8.cloned.1.call-start = ((), (), s32[]{:S(2)}) async-start(), calls=%async_computation.8 | async-start | bytes 2621440 | tf_op jit(solution)/shard_map/all_gather | solution.py:98
  119.2 101.4 %reduce-scatter.5.cloned.1.call-start = ((), (), s32[]{:S(2)}) async-start(), calls=%async_computation.9 | async-start | bytes 2621440 | tf_op jit(solution)/shard_map/reduce_scatter | solution.py:103
  154.6 11.1 %copy-start.5 = (bf16[256,4096]{1,0:T(8,128)(2,1)S(1)}, bf16[256,4096]{1,0:T(8,128)(2,1)}, u32[]{:S(2)}) copy-start(bf16[256,4096]{1,0:T(8,128)(2,1)} %all-gather.8.cloned.1.call-done) | copy-start | bytes 6291460
  165.7 55.0 %copy-start.2 = (bf16[64,4096]{1,0:T(8,128)(2,1)S(1)}, bf16[64,4096]{1,0:T(8,128)(2,1)}, u32[]{:S(2)}) copy-start(bf16[64,4096]{1,0:T(8,128)(2,1)} %reduce-scatter.3.cloned.1.call-done) | copy-start | bytes 1572868
Sparse Core Ops, SparseCore 0:
  16.2 20.4 all-gather.3
  38.3 21.8 all-gather.5
  79.7 36.0 reduce-scatter.2
  119.3 35.1 all-gather.7
  185.4 35.1 reduce-scatter.4
where the time goes:
time: 231 us; the launch traced here: 229 us
  waiting for transfers between devices  137 us (59%)
  matrix products  45.6 us (20%)
  blocking collectives  16.7 us (7%)
  between operations  13.2 us (6%)
  other arithmetic  7.69 us (3%)
  local copies, waits for them, and re-layouts  5.68 us (2%)
  starting transfers between devices  3.76 us (2%)
    reduce_scatter x1, waiting for transfers between devices, local(): lax.psum_scatter(jnp.dot(selected, out_weight, preferred_element_type=jnp...  36.1 us
    reduce_scatter x1, waiting for transfers between devices, local(): lax.psum_scatter(jnp.dot(selected, down_weight, preferred_element_type=jn...  35.3 us
    all_gather x1, waiting for transfers between devices, local(): shard_rows = lax.all_gather(normed, 'head', axis=0, tiled=True)  35.1 us
    all_gather x1, waiting for transfers between devices, local(): value_block = lax.all_gather(value_local, 'blk', axis=0, tiled=True)  23.5 us
    dot_general x1, matrix products, local(): jnp.dot(selected, down_weight, preferred_element_type=jnp.float32)  19.6 us
    dot_general x1, matrix products, local(): jnp.dot(shard_rows, gate_weight, preferred_element_type=jnp.float32)  11.1 us
    all_to_all x1, blocking collectives, local(): lax.all_to_all(key_states, 'head', split_axis=1, concat_axis=0, tiled=True)  8.64 us
    all_to_all x1, blocking collectives, local(): lax.all_to_all(value_states, 'head', split_axis=1, concat_axis=0, tiled=T...  8.07 us
  transfers between devices with their start and end apart: 6, of which 6 were waited for; matrix products, arithmetic and copies ran while one was open for 1% of the time, Pallas kernels for 0%

commit v1 on v0

v1 whole, which is shorter than its diff:
```python
import functools

import jax
import jax.numpy as jnp
from jax import lax
from jax.experimental import pallas as pl
from jax.experimental.pallas import tpu as pltpu
from jax.sharding import PartitionSpec as P

HEADS = 16
KV_HEADS = 8
HEAD_DIM = 128
CHUNKS = 4
MESH = pl.DeviceIdType.MESH
BF = jnp.bfloat16
F32 = jnp.float32


def tile_of(n, most=256):
    t = most
    while n % t:
        t -= 128
    return t


def remote(src, dst, send, recv, axis, index):
    return pltpu.make_async_remote_copy(
        src_ref=src, dst_ref=dst, send_sem=send, recv_sem=recv,
        device_id={axis: index}, device_id_type=MESH,
    )


def kernel(
    H, B,
    hid, q_in, k_in, v_in, gain, wo_h, wg_h, wu_h, wd_h,
    out,
    wo, wg, wu, wd, qb, kv, att, part, rs, gath, accg, accu, inner,
    w_sem, loc_sem, a_s, a_r, z_s, z_r, d_s, d_r, rs_s, rs_r, ag_s, ag_r, r2_s, r2_r,
):
    h = lax.axis_index("head")
    b = lax.axis_index("blk")
    J = B // 2
    j = b // 2
    c = b % 2
    partner = b + 1 - 2 * c
    T = hid.shape[0]
    D = hid.shape[1]
    R = T * H
    QW = qb.shape[1]
    KW = kv.shape[3]
    nh = QW // HEAD_DIM
    ratio = HEADS // KV_HEADS
    CW = D // CHUNKS
    FW = wg.shape[1]

    wcopies = [pltpu.make_async_copy(wo_h, wo, w_sem.at[0])]
    for i in range(CHUNKS):
        rows = pl.ds(i * CW, CW)
        wcopies.append(pltpu.make_async_copy(wg_h.at[rows], wg.at[rows], w_sem.at[1 + 2 * i]))
        wcopies.append(pltpu.make_async_copy(wu_h.at[rows], wu.at[rows], w_sem.at[2 + 2 * i]))
    wcopies.append(pltpu.make_async_copy(wd_h, wd, w_sem.at[1 + 2 * CHUNKS]))
    for w in wcopies:
        w.start()

    barrier = pltpu.get_barrier_semaphore()
    for d in range(1, H):
        pl.semaphore_signal(barrier, inc=1, device_id={"head": lax.rem(h + d, H)}, device_id_type=MESH)
    for d in range(1, J):
        pl.semaphore_signal(barrier, inc=1, device_id={"blk": lax.rem(b + 2 * d, B)}, device_id_type=MESH)
    pl.semaphore_signal(barrier, inc=1, device_id={"blk": partner}, device_id_type=MESH)
    pl.semaphore_wait(barrier, H - 1 + J - 1 + 1)

    my_rows = pl.ds(pl.multiple_of(h * T, T), T)

    def cols(p, w):
        return pl.ds(pl.multiple_of(p * w, w), w)

    a_copies = []
    for t, (src, dst, w) in enumerate(
        ((k_in, kv.at[b, 0], KW), (v_in, kv.at[b, 1], KW), (q_in, qb, QW))
    ):
        for d in range(1, H):
            p = lax.rem(h + d, H)
            cp = remote(
                src.at[:, cols(p, w)], dst.at[my_rows, :],
                a_s.at[d - 1, t], a_r.at[d - 1, t], "head", p,
            )
            cp.start()
            a_copies.append((t, cp))
        lc = pltpu.make_async_copy(src.at[:, cols(h, w)], dst.at[my_rows, :], loc_sem.at[t])
        lc.start()
        a_copies.append((t, lc))

    def wait_in(t):
        for tt, cp in a_copies:
            if tt == t:
                cp.wait()

    def z_copy(slot, t):
        return remote(
            kv.at[slot, t], kv.at[slot, t], z_s.at[slot, t], z_r.at[slot, t],
            "blk", lax.rem(b + 2, B),
        )

    def d_copy(slot, t):
        return remote(
            kv.at[slot, t], kv.at[slot, t], d_s.at[slot, t], d_r.at[slot, t], "blk", partner
        )

    for t in range(2):
        wait_in(t)

        @pl.when(j < J - 1)
        def _():
            z_copy(b, t).start()

        @pl.when(c == 0)
        def _():
            d_copy(b, t).start()

    wait_in(2)

    mq = lambda n: slice(n * HEAD_DIM, (n + 1) * HEAD_DIM)
    ml = lambda n: slice((nh + n) * HEAD_DIM, (nh + n + 1) * HEAD_DIM)
    scale = HEAD_DIM ** (-0.5)

    def absorb(slot, first):
        for n in range(nh):
            g = n // ratio
            s = lax.dot_general(
                qb[:, mq(n)], kv[slot, 0, :, mq(g)],
                (((1,), (1,)), ((), ())), preferred_element_type=F32,
            ) * scale
            if first:
                qi = lax.broadcasted_iota(jnp.int32, s.shape, 0)
                ki = lax.broadcasted_iota(jnp.int32, s.shape, 1)
                s = jnp.where(ki <= qi, s, -1e30)
            top = jnp.max(s, axis=1, keepdims=True)
            if not first:
                old = accu[:, mq(n)][:, :1]
                top = jnp.maximum(top, old)
            e = jnp.exp(s - top)
            tot = jnp.sum(e, axis=1, keepdims=True)
            pv = jnp.dot(e.astype(BF), kv[slot, 1, :, mq(g)], preferred_element_type=F32)
            if not first:
                f = jnp.exp(old - top)
                tot = tot + accu[:, ml(n)][:, :1] * f
                pv = pv + accg[:, mq(n)] * f
            accu[:, mq(n)] = jnp.broadcast_to(top, (R, HEAD_DIM))
            accu[:, ml(n)] = jnp.broadcast_to(tot, (R, HEAD_DIM))
            accg[:, mq(n)] = pv

    absorb(b, True)

    @pl.when(c == 1)
    def _():
        for t in range(2):
            d_copy(b - 1, t).wait_recv()
        absorb(b - 1, False)

    def chain(s, carry):
        slot = 2 * (j - 1 - s) + c
        other = 2 * (j - 1 - s) + 1 - c
        for t in range(2):
            z_copy(slot, t).wait_recv()

            @pl.when(j < J - 1)
            def _():
                z_copy(slot, t).start()

            d_copy(slot, t).start()
        absorb(slot, False)
        for t in range(2):
            d_copy(other, t).wait_recv()
        absorb(other, False)
        return carry

    lax.fori_loop(0, j, chain, 0)

    for n in range(nh):
        att[:, mq(n)] = (accg[:, mq(n)] / accu[:, ml(n)]).astype(BF)

    def scatter(w_ref, x_ref, send, recv):
        copies = []
        ct = tile_of(CW)
        for i in range(CHUNKS):
            def step(t, carry):
                cs = pl.ds(pl.multiple_of(i * CW + t * ct, ct), ct)
                part[:, cs] = jnp.dot(
                    x_ref[...], w_ref[:, cs], preferred_element_type=F32
                ).astype(BF)
                return carry

            lax.fori_loop(0, CW // ct, step, 0)
            cs = pl.ds(i * CW, CW)
            for d in range(1, H):
                p = lax.rem(h + d, H)
                cp = remote(
                    part.at[pl.ds(pl.multiple_of(p * T, T), T), cs], rs.at[d - 1, :, cs],
                    send.at[d - 1, i], recv.at[d - 1, i], "head", p,
                )
                cp.start()
                copies.append(cp)
        return copies

    def reduced(i, copies):
        cs = pl.ds(i * CW, CW)
        for d in range(1, H):
            copies[i * (H - 1) + d - 1].wait_recv()
        total = part[my_rows, cs].astype(F32)
        for d in range(1, H):
            total = total + rs[d - 1, :, cs].astype(F32)
        return total

    wcopies[0].wait()
    rs_copies = scatter(wo, att, rs_s, rs_r)
    ag_copies = []
    for i in range(CHUNKS):
        cs = pl.ds(i * CW, CW)
        gath[my_rows, cs] = (hid[:, cs].astype(F32) + reduced(i, rs_copies)).astype(BF)
        for d in range(1, H):
            cp = remote(
                gath.at[my_rows, cs], gath.at[my_rows, cs],
                ag_s.at[d - 1, i], ag_r.at[d - 1, i], "head", lax.rem(h + d, H),
            )
            cp.start()
            ag_copies.append(cp)

    ft = tile_of(FW)
    square = jnp.zeros((R, 1), F32)
    for i in range(CHUNKS):
        cs = pl.ds(i * CW, CW)
        for d in range(1, H):
            ag_copies[i * (H - 1) + d - 1].wait_recv()
        wcopies[1 + 2 * i].wait()
        wcopies[2 + 2 * i].wait()
        x = gath[:, cs].astype(F32)
        square = square + jnp.sum(x * x, axis=1, keepdims=True)
        xg = (x * gain[:, cs]).astype(BF)

        def step(t, carry, xg=xg, cs=cs, i=i):
            fs = pl.ds(pl.multiple_of(t * ft, ft), ft)
            g = jnp.dot(xg, wg[cs, fs], preferred_element_type=F32)
            u = jnp.dot(xg, wu[cs, fs], preferred_element_type=F32)
            if i:
                g = g + accg[:, fs]
                u = u + accu[:, fs]
            accg[:, fs] = g
            accu[:, fs] = u
            return carry

        lax.fori_loop(0, FW // ft, step, 0)
    r = lax.rsqrt(square / D + 1e-5)

    def act(t, carry):
        fs = pl.ds(pl.multiple_of(t * ft, ft), ft)
        g = accg[:, fs] * r
        u = accu[:, fs] * r
        inner[:, fs] = (g / (1.0 + jnp.exp(-g)) * u).astype(BF)
        return carry

    lax.fori_loop(0, FW // ft, act, 0)
    for cp in rs_copies:
        cp.wait_send()
    wcopies[-1].wait()
    r2_copies = scatter(wd, inner, r2_s, r2_r)
    for i in range(CHUNKS):
        cs = pl.ds(i * CW, CW)
        out[:, cs] = (gath[my_rows, cs].astype(F32) + reduced(i, r2_copies)).astype(BF)

    for cp in ag_copies + r2_copies:
        cp.wait_send()
    for t in range(2):
        @pl.when(j < J - 1)
        def _():
            z_copy(b, t).wait_send()

        @pl.when(c == 0)
        def _():
            d_copy(b, t).wait_send()

    def drain(s, carry):
        slot = 2 * (j - 1 - s) + c
        for t in range(2):
            @pl.when(j < J - 1)
            def _():
                z_copy(slot, t).wait_send()

            d_copy(slot, t).wait_send()
        return carry

    lax.fori_loop(0, j, drain, 0)


def solution(mesh):
    H = mesh.shape["head"]
    B = mesh.shape["blk"]

    def local(hid, q, k, v, wo, gain, wg, wu, wd):
        T, D = hid.shape
        R = T * H
        QW = q.shape[1] // H
        KW = k.shape[1] // H
        FW = wg.shape[1]
        vm = pl.BlockSpec(memory_space=pltpu.VMEM)
        hbm = pl.BlockSpec(memory_space=pl.ANY)
        dma = pltpu.SemaphoreType.DMA
        return pl.pallas_call(
            functools.partial(kernel, H, B),
            out_shape=jax.ShapeDtypeStruct((T, D), BF),
            in_specs=[vm] * 5 + [hbm] * 4,
            out_specs=vm,
            scratch_shapes=[
                pltpu.VMEM(wo.shape, BF),
                pltpu.VMEM(wg.shape, BF),
                pltpu.VMEM(wu.shape, BF),
                pltpu.VMEM(wd.shape, BF),
                pltpu.VMEM((R, QW), BF),
                pltpu.VMEM((B, 2, R, KW), BF),
                pltpu.VMEM((R, QW), BF),
                pltpu.VMEM((R, D), BF),
                pltpu.VMEM((H - 1, T, D), BF),
                pltpu.VMEM((R, D), BF),
                pltpu.VMEM((R, FW), F32),
                pltpu.VMEM((R, FW), F32),
                pltpu.VMEM((R, FW), BF),
                dma((2 + 2 * CHUNKS,)),
                dma((3,)),
                dma((H - 1, 3)), dma((H - 1, 3)),
                dma((B, 2)), dma((B, 2)),
                dma((B, 2)), dma((B, 2)),
                dma((H - 1, CHUNKS)), dma((H - 1, CHUNKS)),
                dma((H - 1, CHUNKS)), dma((H - 1, CHUNKS)),
                dma((H - 1, CHUNKS)), dma((H - 1, CHUNKS)),
            ],
            compiler_params=pltpu.CompilerParams(
                collective_id=0, has_side_effects=True, vmem_limit_bytes=67_043_328
            ),
        )(hid, q, k, v, gain.reshape(1, -1), wo, wg, wu, wd)

    rows = P(("blk", "head"), None)
    return jax.shard_map(
        local,
        mesh=mesh,
        in_specs=(rows, rows, rows, rows, P("head", None), P(), P(None, "head"), P(None, "head"), P("head", None)),
        out_specs=rows,
        check_vma=False,
    )
```

time: 231 us -> 113 us (0.49)
  waiting for transfers between devices: 137 us -> 0 us
  Pallas kernels: 0 us -> 110 us
  matrix products: 45.6 us -> 0 us
  blocking collectives: 16.7 us -> 0 us
  between operations: 13.2 us -> 0.01 us
  other arithmetic: 7.69 us -> 0 us
  local copies, waits for them, and re-layouts: 5.68 us -> 1.87 us
  starting transfers between devices: 3.76 us -> 0 us
    pallas_call x0 -> x1, Pallas kernels: none -> 110 us  [local(): pl.pallas_call(functools.partial(kernel, H, B), out_shape=jax.ShapeDtypeS...]
    reduce_scatter x2 -> x0, waiting for transfers between devices: 71.5 us -> none  [the longest x1 36.1 us: local(): lax.psum_scatter(jnp.dot(selected, out_weight, preferred_element_type=jnp...]
    all_gather x3 -> x0, waiting for transfers between devices: 59.7 us -> none  [the longest x1 35.1 us: local(): shard_rows = lax.all_gather(normed, 'head', axis=0, tiled=True)]
    dot_general x4 -> x0, matrix products: 40.3 us -> none  [the longest x1 19.6 us: local(): jnp.dot(selected, down_weight, preferred_element_type=jnp.float32)]
    all_to_all x2 -> x0, blocking collectives: 16.7 us -> none  [the longest x1 8.64 us: local(): lax.all_to_all(key_states, 'head', split_axis=1, concat_axis=0, tiled=True)]
    cond x1 -> x0, matrix products: 5.31 us -> none  [local(): lax.cond(jnp.int32(0) > last_query, skipped, worked, start_state)]
    all_to_all x1 -> x0, waiting for transfers between devices: 5.28 us -> none  [local(): lax.all_to_all(queries, 'head', split_axis=1, concat_axis=0, tiled=True)]
    convert_element_type x3 -> x0, other arithmetic: 4.11 us -> none  [the longest x1 2.04 us: local(): (widened * lax.rsqrt(mean_square + 1e-05) * norm_gain).astype(jnp.bfloat16)]
  transfers between devices with their start and end apart: 6 -> 0, of which waited for: 6 -> 0; matrix products, arithmetic and copies ran while one was open for 1% -> 0% of each run, Pallas kernels for 0% -> 0%
where the time goes in v1:
time: 113 us; the launch traced here: 112 us
  Pallas kernels  110 us (97%)
  local copies, waits for them, and re-layouts  1.87 us (2%)
    pallas_call x1, Pallas kernels, local(): pl.pallas_call(functools.partial(kernel, H, B), out_shape=jax.ShapeDtypeS...  110 us

profile of v1, /device:TPU:24, one launch (start us, length us, event | category | flops | bytes accessed | tf_op | source)
XLA Modules:
  0.0 112.3 jit_solution(6945855770854563474)
XLA Ops:
  0.0 110.4 %shard_map.91 = bf16[64,4096]{1,0:T(8,128)(2,1)} custom-call(bf16[64,4096]{1,0:T(8,128)(2,1)} %hid.1, bf16[64,2048]{1,0:T(8,128)(2,1)} %q_in.1, bf16[64,1024]{1,0:T(8,128)(2,1)} %k_in.1, bf16[64,1024]{1,0:T(8,128)(2,1)} %v_in.1, f32[1,4096]{1,0:T(1,128)} %bitcast.1, bf16[512,4096]{1,0:T(8,128)(2,1)} %wo_h.1, bf16[4096,1792]{1,0:T(8,128)(2,1)} %wg_h.1, ...), custom_call_target="tpu_custom_call" | custom-call | tf_op jit(solution)/shard_map/pallas_call | solution.py:308
  110.4 1.9 %copy.11 = bf16[64,4096]{1,0:T(8,128)(2,1)} copy(bf16[64,4096]{1,0:T(8,128)(2,1)} %shard_map.91) | data formatting | bytes 1048576

commit v2 on v1

--- a/solution.py
+++ b/solution.py
@@ -180,8 +180,20 @@
     for n in range(nh):
         att[:, mq(n)] = (accg[:, mq(n)] / accu[:, ml(n)]).astype(BF)
 
+    square_ring = H == 4
+    nx = h + 1 - 2 * (h % 2)
+    ny = lax.rem(h + H // 2, H)
+    dg = H - 1 - h
+    HW = CW // 2
+
+    def rows_of(p):
+        return pl.ds(pl.multiple_of(p * T, T), T)
+
+    def halves(i):
+        return pl.ds(i * CW, HW), pl.ds(i * CW + HW, HW)
+
     def scatter(w_ref, x_ref, send, recv):
-        copies = []
+        copies = {}
         ct = tile_of(CW)
         for i in range(CHUNKS):
             def step(t, carry):
@@ -192,57 +204,97 @@
                 return carry
 
             lax.fori_loop(0, CW // ct, step, 0)
-            cs = pl.ds(i * CW, CW)
-            for d in range(1, H):
-                p = lax.rem(h + d, H)
+            if square_ring:
+                ha, hb = halves(i)
+                plan = ((1, dg, ha, 0, nx), (1, dg, hb, 1, ny), (0, nx, ha, 2, nx), (0, ny, hb, 3, ny))
+            else:
+                cs = pl.ds(i * CW, CW)
+                plan = [(d - 1, lax.rem(h + d, H), cs, d - 1, lax.rem(h + d, H)) for d in range(1, H)]
+            for place, block, cs, sem, to in plan:
                 cp = remote(
-                    part.at[pl.ds(pl.multiple_of(p * T, T), T), cs], rs.at[d - 1, :, cs],
-                    send.at[d - 1, i], recv.at[d - 1, i], "head", p,
+                    part.at[rows_of(block), cs], rs.at[place, :, cs],
+                    send.at[sem, i], recv.at[sem, i], "head", to,
                 )
                 cp.start()
-                copies.append(cp)
+                copies[sem, i] = cp
         return copies
+
+    def combine(i, copies, send, recv):
+        if not square_ring:
+            return
+        ha, hb = halves(i)
+        for cs, sem, to in ((ha, 0, ny), (hb, 1, nx)):
+            copies[sem, i].wait_recv()
+            blk_rows = rows_of(to)
+            part[blk_rows, cs] = (
+                part[blk_rows, cs].astype(F32) + rs[1, :, cs].astype(F32)
+            ).astype(BF)
+            cp = remote(
+                part.at[blk_rows, cs], rs.at[2, :, cs],
+                send.at[4 + sem, i], recv.at[4 + sem, i], "head", to,
+            )
+            cp.start()
+            copies[4 + sem, i] = cp
 
     def reduced(i, copies):
         cs = pl.ds(i * CW, CW)
-        for d in range(1, H):
-            copies[i * (H - 1) + d - 1].wait_recv()
+        sems = (2, 3, 4, 5) if square_ring else range(H - 1)
+        for sem in sems:
+            copies[sem, i].wait_recv()
         total = part[my_rows, cs].astype(F32)
-        for d in range(1, H):
-            total = total + rs[d - 1, :, cs].astype(F32)
+        for place in (0, 2) if square_ring else range(H - 1):
+            total = total + rs[place, :, cs].astype(F32)
         return total
 
     wcopies[0].wait()
     rs_copies = scatter(wo, att, rs_s, rs_r)
-    ag_copies = []
-    for i in range(CHUNKS):
-        cs = pl.ds(i * CW, CW)
-        gath[my_rows, cs] = (hid[:, cs].astype(F32) + reduced(i, rs_copies)).astype(BF)
-        for d in range(1, H):
-            cp = remote(
-                gath.at[my_rows, cs], gath.at[my_rows, cs],
-                ag_s.at[d - 1, i], ag_r.at[d - 1, i], "head", lax.rem(h + d, H),
-            )
-            cp.start()
-            ag_copies.append(cp)
+    ag_copies = {}
+
+    def spread(rows, cs, sem, i, to):
+        cp = remote(
+            gath.at[rows, cs], gath.at[rows, cs],
+            ag_s.at[sem, i], ag_r.at[sem, i], "head", to,
+        )
+        cp.start()
+        ag_copies[sem, i] = cp
+
+    for i in range(CHUNKS + 1):
+        if i < CHUNKS:
+            combine(i, rs_copies, rs_s, rs_r)
+        if i:
+            cs = pl.ds((i - 1) * CW, CW)
+            gath[my_rows, cs] = (hid[:, cs].astype(F32) + reduced(i - 1, rs_copies)).astype(BF)
+            for sem, to in enumerate(
+                (nx, ny) if square_ring else [lax.rem(h + d, H) for d in range(1, H)]
+            ):
+                spread(my_rows, cs, sem, i - 1, to)
 
     ft = tile_of(FW)
     square = jnp.zeros((R, 1), F32)
-    for i in range(CHUNKS):
-        cs = pl.ds(i * CW, CW)
-        for d in range(1, H):
-            ag_copies[i * (H - 1) + d - 1].wait_recv()
-        wcopies[1 + 2 * i].wait()
-        wcopies[2 + 2 * i].wait()
+    for i in range(CHUNKS + 1):
+        if i < CHUNKS and square_ring:
+            ha, hb = halves(i)
+            ag_copies[0, i].wait_recv()
+            spread(rows_of(nx), ha, 2, i, ny)
+            ag_copies[1, i].wait_recv()
+            spread(rows_of(ny), hb, 3, i, nx)
+        if i == 0:
+            continue
+        k = i - 1
+        cs = pl.ds(k * CW, CW)
+        for sem in (2, 3) if square_ring else range(H - 1):
+            ag_copies[sem, k].wait_recv()
+        wcopies[1 + 2 * k].wait()
+        wcopies[2 + 2 * k].wait()
         x = gath[:, cs].astype(F32)
         square = square + jnp.sum(x * x, axis=1, keepdims=True)
         xg = (x * gain[:, cs]).astype(BF)
 
-        def step(t, carry, xg=xg, cs=cs, i=i):
+        def step(t, carry, xg=xg, cs=cs, k=k):
             fs = pl.ds(pl.multiple_of(t * ft, ft), ft)
             g = jnp.dot(xg, wg[cs, fs], preferred_element_type=F32)
             u = jnp.dot(xg, wu[cs, fs], preferred_element_type=F32)
-            if i:
+            if k:
                 g = g + accg[:, fs]
                 u = u + accu[:, fs]
             accg[:, fs] = g
@@ -260,15 +312,18 @@
         return carry
 
     lax.fori_loop(0, FW // ft, act, 0)
-    for cp in rs_copies:
+    for cp in rs_copies.values():
         cp.wait_send()
     wcopies[-1].wait()
     r2_copies = scatter(wd, inner, r2_s, r2_r)
-    for i in range(CHUNKS):
-        cs = pl.ds(i * CW, CW)
-        out[:, cs] = (gath[my_rows, cs].astype(F32) + reduced(i, r2_copies)).astype(BF)
-
-    for cp in ag_copies + r2_copies:
+    for i in range(CHUNKS + 1):
+        if i < CHUNKS:
+            combine(i, r2_copies, r2_s, r2_r)
+        if i:
+            cs = pl.ds((i - 1) * CW, CW)
+            out[:, cs] = (gath[my_rows, cs].astype(F32) + reduced(i - 1, r2_copies)).astype(BF)
+
+    for cp in (*ag_copies.values(), *r2_copies.values()):
         cp.wait_send()
     for t in range(2):
         @pl.when(j < J - 1)
@@ -329,9 +384,9 @@
                 dma((H - 1, 3)), dma((H - 1, 3)),
                 dma((B, 2)), dma((B, 2)),
                 dma((B, 2)), dma((B, 2)),
-                dma((H - 1, CHUNKS)), dma((H - 1, CHUNKS)),
-                dma((H - 1, CHUNKS)), dma((H - 1, CHUNKS)),
-                dma((H - 1, CHUNKS)), dma((H - 1, CHUNKS)),
+                dma((max(H - 1, 6), CHUNKS)), dma((max(H - 1, 6), CHUNKS)),
+                dma((max(H - 1, 6), CHUNKS)), dma((max(H - 1, 6), CHUNKS)),
+                dma((max(H - 1, 6), CHUNKS)), dma((max(H - 1, 6), CHUNKS)),
             ],
             compiler_params=pltpu.CompilerParams(
                 collective_id=0, has_side_effects=True, vmem_limit_bytes=67_043_328

time: 113 us -> 103 us (0.912)
  Pallas kernels: 110 us -> 101 us
    pallas_call x1, Pallas kernels: 110 us -> 101 us  [local(): pl.pallas_call(functools.partial(kernel, H, B), out_shape=jax.ShapeDtypeS...]
where the time goes in v2:
time: 103 us
  Pallas kernels  101 us (98%)
  local copies, waits for them, and re-layouts  1.87 us (2%)
    pallas_call x1, Pallas kernels, local(): pl.pallas_call(functools.partial(kernel, H, B), out_shape=jax.ShapeDtypeS...  101 us

profile of v2, /device:TPU:24, one launch (start us, length us, event | category | flops | bytes accessed | tf_op | source)
XLA Modules:
  0.0 103.0 jit_solution(16557815673011908641)
XLA Ops:
  0.0 101.2 %shard_map.91 = bf16[64,4096]{1,0:T(8,128)(2,1)} custom-call(bf16[64,4096]{1,0:T(8,128)(2,1)} %hid.1, bf16[64,2048]{1,0:T(8,128)(2,1)} %q_in.1, bf16[64,1024]{1,0:T(8,128)(2,1)} %k_in.1, bf16[64,1024]{1,0:T(8,128)(2,1)} %v_in.1, f32[1,4096]{1,0:T(1,128)} %bitcast.1, bf16[512,4096]{1,0:T(8,128)(2,1)} %wo_h.1, bf16[4096,1792]{1,0:T(8,128)(2,1)} %wg_h.1, ...), custom_call_target="tpu_custom_call" | custom-call | tf_op jit(solution)/shard_map/pallas_call | solution.py:363
  101.2 1.9 %copy.11 = bf16[64,4096]{1,0:T(8,128)(2,1)} copy(bf16[64,4096]{1,0:T(8,128)(2,1)} %shard_map.91) | data formatting | bytes 1048576

commit v3 on v2

--- a/solution.py
+++ b/solution.py
@@ -11,6 +11,7 @@
 KV_HEADS = 8
 HEAD_DIM = 128
 CHUNKS = 4
+AHEAD = 2
 MESH = pl.DeviceIdType.MESH
 BF = jnp.bfloat16
 F32 = jnp.float32
@@ -59,16 +60,20 @@
         wcopies.append(pltpu.make_async_copy(wg_h.at[rows], wg.at[rows], w_sem.at[1 + 2 * i]))
         wcopies.append(pltpu.make_async_copy(wu_h.at[rows], wu.at[rows], w_sem.at[2 + 2 * i]))
     wcopies.append(pltpu.make_async_copy(wd_h, wd, w_sem.at[1 + 2 * CHUNKS]))
-    for w in wcopies:
-        w.start()
-
     barrier = pltpu.get_barrier_semaphore()
     for d in range(1, H):
         pl.semaphore_signal(barrier, inc=1, device_id={"head": lax.rem(h + d, H)}, device_id_type=MESH)
-    for d in range(1, J):
-        pl.semaphore_signal(barrier, inc=1, device_id={"blk": lax.rem(b + 2 * d, B)}, device_id_type=MESH)
+
+    @pl.when(j > 0)
+    def _():
+        pl.semaphore_signal(barrier, inc=1, device_id={"blk": lax.rem(b + B - 2, B)}, device_id_type=MESH)
+
+    @pl.when(j < J - 1)
+    def _():
+        pl.semaphore_signal(barrier, inc=1, device_id={"blk": lax.rem(b + 2, B)}, device_id_type=MESH)
+
     pl.semaphore_signal(barrier, inc=1, device_id={"blk": partner}, device_id_type=MESH)
-    pl.semaphore_wait(barrier, H - 1 + J - 1 + 1)
+    pl.semaphore_wait(barrier, H + jnp.minimum(j, 1) + jnp.minimum(J - 1 - j, 1))
 
     my_rows = pl.ds(pl.multiple_of(h * T, T), T)
 
@@ -119,6 +124,8 @@
             d_copy(b, t).start()
 
     wait_in(2)
+    for w in wcopies:
+        w.start()
 
     mq = lambda n: slice(n * HEAD_DIM, (n + 1) * HEAD_DIM)
     ml = lambda n: slice((nh + n) * HEAD_DIM, (nh + n + 1) * HEAD_DIM)
@@ -258,16 +265,20 @@
         cp.start()
         ag_copies[sem, i] = cp
 
+    def spread_own(i):
+        for sem, to in enumerate(
+            (nx, ny) if square_ring else [lax.rem(h + d, H) for d in range(1, H)]
+        ):
+            spread(my_rows, pl.ds(i * CW, CW), sem, i, to)
+
     for i in range(CHUNKS + 1):
         if i < CHUNKS:
             combine(i, rs_copies, rs_s, rs_r)
         if i:
             cs = pl.ds((i - 1) * CW, CW)
             gath[my_rows, cs] = (hid[:, cs].astype(F32) + reduced(i - 1, rs_copies)).astype(BF)
-            for sem, to in enumerate(
-                (nx, ny) if square_ring else [lax.rem(h + d, H) for d in range(1, H)]
-            ):
-                spread(my_rows, cs, sem, i - 1, to)
+            if i <= AHEAD or not square_ring:
+                spread_own(i - 1)
 
     ft = tile_of(FW)
     square = jnp.zeros((R, 1), F32)
@@ -278,6 +289,8 @@
             spread(rows_of(nx), ha, 2, i, ny)
             ag_copies[1, i].wait_recv()
             spread(rows_of(ny), hb, 3, i, nx)
+            if i + AHEAD < CHUNKS:
+                spread_own(i + AHEAD)
         if i == 0:
             continue
         k = i - 1

time: 103 us -> 99.5 us (0.966)
  Pallas kernels: 101 us -> 97.4 us
    pallas_call x1, Pallas kernels: 101 us -> 97.4 us  [local(): pl.pallas_call(functools.partial(kernel, H, B), out_shape=jax.ShapeDtypeS...]
where the time goes in v3:
time: 99.5 us; the launch traced here: 99.3 us
  Pallas kernels  97.4 us (98%)
  local copies, waits for them, and re-layouts  1.87 us (2%)
    pallas_call x1, Pallas kernels, local(): pl.pallas_call(functools.partial(kernel, H, B), out_shape=jax.ShapeDtypeS...  97.4 us

profile of v3, /device:TPU:24, one launch (start us, length us, event | category | flops | bytes accessed | tf_op | source)
XLA Modules:
  0.0 99.3 jit_solution(18370081841283751491)
XLA Ops:
  0.0 97.4 %shard_map.91 = bf16[64,4096]{1,0:T(8,128)(2,1)} custom-call(bf16[64,4096]{1,0:T(8,128)(2,1)} %hid.1, bf16[64,2048]{1,0:T(8,128)(2,1)} %q_in.1, bf16[64,1024]{1,0:T(8,128)(2,1)} %k_in.1, bf16[64,1024]{1,0:T(8,128)(2,1)} %v_in.1, f32[1,4096]{1,0:T(1,128)} %bitcast.1, bf16[512,4096]{1,0:T(8,128)(2,1)} %wo_h.1, bf16[4096,1792]{1,0:T(8,128)(2,1)} %wg_h.1, ...), custom_call_target="tpu_custom_call" | custom-call | tf_op jit(solution)/shard_map/pallas_call | solution.py:376
  97.4 1.9 %copy.11 = bf16[64,4096]{1,0:T(8,128)(2,1)} copy(bf16[64,4096]{1,0:T(8,128)(2,1)} %shard_map.91) | data formatting | bytes 1048576
